TPU v7x, 32 devices: a whole 2x2x4 slice. The times are simulated.
32 devices in a mesh: pool: 16 (over z, y, x), serve: 2 (over core).
Axes of the slice: x: 2, y: 2, z: 4, core: 2. Of those that a mesh axis runs over, the one named last changes fastest.
Arguments:
- queries: bfloat16 [2, 256, 73728], P('serve', None, 'pool'), may hold values from -16 to 16
- new_latent: bfloat16 [2, 147456], P('serve', 'pool'), may hold values from -8 to 8
- pool: bfloat16 [2, 192, 36864], P('serve', 'pool'), may hold values from -6 to 6
- page_owner: int32 [2, 32], P('serve'), may hold values from 0 to 15, as said below
- page_slot: int32 [2, 32], P('serve'), may hold values from 0 to 10
- new_owner: int32 [2, 4], P('serve'), may hold values from 0 to 15, as said below
- new_slot: int32 [2, 4], P('serve'), may hold values from 0 to 11
- prefix_len: int32 [2], P('serve'), may hold values from 512 to 2048, as said below
- w_uv: bfloat16 [128, 512, 128], P('pool', 'serve'), may hold values from -1 to 1
Outputs:
- attn_out: bfloat16 [2, 256, 16384], P('serve', None, 'pool')
- new_pool: bfloat16 [2, 192, 36864], P('serve', 'pool')
Inputs may be any that keep to these rules, and one draw needn't show every extreme that they name: Within a request the pairs (page_owner, page_slot) differ from one another and from the pairs (new_owner, new_slot); at most 3 entries of a request's table name the same owner, and in every request some owner is named exactly 3 times. `new_owner`: the 4 new pages of a request go to different owners. `prefix_len`: some request has exactly 2048 prefix tokens.
All inputs are finite; a program needn't handle non-finite values.
Results may differ from a plain program's by a relative error of at most 0.0075.
Values may be sent and summed in bfloat16 or wider, within the bound.
A program may use at most 128 MiB of HBM per device.

v0:
```python
import functools

import jax
import jax.numpy as jnp
from jax import lax
from jax.experimental import pallas as pl
from jax.experimental.pallas import tpu as pltpu
from jax.sharding import PartitionSpec as P

VLAT = 512
VHEAD = 128
PAGE = 64
SUF = 256
HOT = 3
LAT = 576
PPAGES = 32
NEWP = 4
SLOTS = 12

LANES = 128
ROPE = LAT - VLAT
PAGE_ROWS = PAGE * LAT // LANES
KEYS = PPAGES * PAGE + SUF
WIDE = 640

softmax_scale = 192.0 ** (-0.5)
masked_score = -1e30
exp2_scale = softmax_scale * 1.4426950408889634

MESH = pl.DeviceIdType.MESH


def fused_kernel(n, serve_n, tokens, block_ref, w_ref, q_ref, count_ref, out_ref, suffix_ref,
                 g_ref, wg_ref, qs_ref, k_ref, stage_ref, acc_ref, top_ref, sum_ref,
                 z_send, z_recv, x_send, x_recv, y_send, y_recv, w_send, w_recv):
    depth = n // 4
    heads = q_ref.shape[1] // LAT
    half = block_ref.shape[0] // 2
    me = lax.axis_index("pool")
    core = lax.axis_index("serve")
    x = me % 2
    y = (me // 2) % 2
    z = me // 4
    x_peer = z * 4 + y * 2 + (1 - x)
    y_peer = z * 4 + (1 - y) * 2 + x

    barrier = pltpu.get_barrier_semaphore()
    for d in range(1, depth):
        there = ((z + d) % depth) * 4 + y * 2 + x
        pl.semaphore_signal(barrier, inc=1, device_id={"pool": there}, device_id_type=MESH)
    pl.semaphore_signal(barrier, inc=1, device_id={"pool": x_peer}, device_id_type=MESH)
    pl.semaphore_signal(barrier, inc=1, device_id={"pool": y_peer}, device_id_type=MESH)
    for d in range(1, serve_n):
        pl.semaphore_signal(
            barrier, inc=1, device_id={"serve": (core + d) % serve_n}, device_id_type=MESH
        )
    pl.semaphore_wait(barrier, depth + serve_n)

    started = []

    def send(src, dst, send_sem, recv_sem, device_id):
        copy = pltpu.make_async_remote_copy(
            src_ref=src, dst_ref=dst, send_sem=send_sem, recv_sem=recv_sem,
            device_id=device_id, device_id_type=MESH,
        )
        copy.start()
        started.append(copy)
        return copy

    order = []
    for d in range(1, depth // 2 + 1):
        order.append(d)
        if depth - d != d:
            order.append(depth - d)

    def base_of(d):
        return ((z - d + depth) % depth) * 4

    def part(ref, i):
        return ref.at[pl.ds(i * half, half)]

    arrivals = {}

    def spread(d):
        owner = base_of(d) + y * 2 + x
        src = block_ref if d == 0 else g_ref.at[owner]
        dst = g_ref.at[owner]
        arrivals[d] = [
            send(part(src, 0), part(dst, 0), x_send.at[d, 0], x_recv.at[d, 0], {"pool": x_peer}),
            send(part(src, 1), part(dst, 1), y_send.at[d, 0], y_recv.at[d, 0], {"pool": y_peer}),
            send(part(src, 1), part(dst, 1), x_send.at[d, 1], x_recv.at[d, 1], {"pool": x_peer}),
            send(part(src, 0), part(dst, 0), y_send.at[d, 1], y_recv.at[d, 1], {"pool": y_peer}),
        ]

    def forward(d):
        x_first, y_first, x_second, y_second = arrivals[d]
        x_first.wait_recv()
        over = part(g_ref.at[base_of(d) + y * 2 + (1 - x)], 0)
        to_y = send(over, over, y_send.at[d, 2], y_recv.at[d, 2], {"pool": y_peer})
        y_first.wait_recv()
        over = part(g_ref.at[base_of(d) + (1 - y) * 2 + x], 1)
        to_x = send(over, over, x_send.at[d, 2], x_recv.at[d, 2], {"pool": x_peer})
        arrivals[d] = [x_second, y_second, to_y, to_x]

    spread(0)
    z_copies = {}
    for d in order:
        there = ((z + d) % depth) * 4 + y * 2 + x
        z_copies[d] = send(block_ref, g_ref.at[me], z_send.at[d], z_recv.at[d], {"pool": there})
    w_copies = [
        send(w_ref, wg_ref.at[core], w_send.at[d], w_recv.at[d], {"serve": (core + d) % serve_n})
        for d in range(1, serve_n)
    ]

    pending = []

    def advance(d):
        def step():
            z_copies[d].wait_recv()
            spread(d)
        return step

    pending.append(lambda: forward(0))
    for d in order:
        pending.append(advance(d))
        pending.append(functools.partial(forward, d))

    def communicate(steps):
        for _ in range(min(steps, len(pending))):
            pending.pop(0)()

    g_ref[pl.ds(me, 1)] = block_ref[...][None]
    wg_ref[pl.ds(core, 1)] = w_ref[...][None]
    unit = jnp.where(
        lax.broadcasted_iota(jnp.int32, (SUF, WIDE - LAT), 1) == 0, 1.0, 0.0
    ).astype(jnp.bfloat16)
    for h in range(heads):
        qs_ref[h * SUF:(h + 1) * SUF, :] = jnp.concatenate(
            [q_ref[:, h * LAT:(h + 1) * LAT], unit], axis=1
        )

    lane = lax.broadcasted_iota(jnp.int32, (PAGE // 2, LANES), 1)
    line = lax.broadcasted_iota(jnp.int32, (PAGE // 2, LANES), 0)

    def unpack(d):
        def place(i, carry):
            owner = base_of(d) + i // HOT
            rank = i % HOT
            base = pl.multiple_of(rank * PAGE_ROWS, 16)
            row = pl.multiple_of(i * PAGE, PAGE)
            for c in range(VLAT // LANES):
                k_ref[pl.ds(row, PAGE), c * LANES:(c + 1) * LANES] = g_ref[
                    owner, pl.ds(base + c * PAGE, PAGE), :]
            rope = g_ref[owner, pl.ds(base + PAGE * VLAT // LANES, PAGE // 2), :].astype(jnp.float32)
            count = count_ref[owner * HOT + rank]
            swapped = jnp.concatenate([rope[:, ROPE:], rope[:, :ROPE]], axis=1)
            for k, values in enumerate((rope, swapped)):
                absent = (lane == ROPE) & (line + k * (PAGE // 2) >= count)
                tile = jnp.where(lane < ROPE, values, jnp.where(absent, masked_score, 0.0))
                k_ref[pl.ds(row + k * (PAGE // 2), PAGE // 2), VLAT:WIDE] = tile.astype(jnp.bfloat16)
            return carry

        lax.fori_loop(0, 4 * HOT, place, 0)

    tile_rows = 2 * SUF
    tiles = heads // 2
    contract_last = (((1,), (1,)), ((), ()))

    def absorb(keys_ref, low, high, first, causal):
        def tile(t, carry):
            rows = pl.ds(pl.multiple_of(t * tile_rows, tile_rows), tile_rows)
            keys = keys_ref[...]
            scores = lax.dot_general(
                qs_ref[rows, :], keys, contract_last, preferred_element_type=jnp.float32
            )
            if causal:
                row = lax.broadcasted_iota(jnp.int32, scores.shape, 0) % SUF
                col = lax.broadcasted_iota(jnp.int32, scores.shape, 1)
                scores = jnp.where(col <= row, scores, masked_score)
            top = jnp.max(scores, axis=1, keepdims=True)
            if not first:
                before = top_ref[rows, :1]
                top = jnp.maximum(top, before)
            shift = top * exp2_scale
            weights = jnp.exp2(scores * exp2_scale - shift)
            total = jnp.sum(weights, axis=1, keepdims=True)
            mixed = jnp.dot(
                weights.astype(jnp.bfloat16), keys[:, :VLAT], preferred_element_type=jnp.float32
            )
            if not first:
                rescale = jnp.exp2((before - top) * exp2_scale)
                total = total + sum_ref[rows, :1] * rescale
                mixed = mixed + acc_ref[rows, :] * rescale
            top_ref[rows, :] = jnp.broadcast_to(top, (tile_rows, LANES))
            sum_ref[rows, :] = jnp.broadcast_to(total, (tile_rows, LANES))
            acc_ref[rows, :] = mixed
            return carry

        lax.fori_loop(low, high, tile, 0)

    communicate(2)
    for k, d in enumerate([0] + order):
        while len(arrivals[d]) != 4 or (len(pending) > 2 * (len(order) - k) and pending):
            communicate(1)
        for copy in arrivals[d]:
            copy.wait_recv()
        unpack(d)
        absorb(k_ref, 0, tiles // 2, k == 0, False)
        communicate(2)
        absorb(k_ref, tiles // 2, tiles, k == 0, False)
        communicate(2)

    base = HOT * PAGE_ROWS

    def place_suffix(o, carry):
        rows = pl.ds(pl.multiple_of(o * tokens, 8), tokens)
        for c in range(VLAT // LANES):
            stage_ref[rows, c * LANES:(c + 1) * LANES] = g_ref[
                o, base + c * tokens:base + (c + 1) * tokens, :].astype(jnp.float32)
        at = base + tokens * VLAT // LANES
        rope = g_ref[o, at:at + tokens // 2, :].astype(jnp.float32)
        swapped = jnp.concatenate([rope[:, ROPE:], rope[:, :ROPE]], axis=1)
        both = jnp.concatenate([rope, swapped], axis=0)
        keep = lax.broadcasted_iota(jnp.int32, (tokens, LANES), 1) < ROPE
        stage_ref[rows, VLAT:WIDE] = jnp.where(keep, both, 0.0)
        return carry

    lax.fori_loop(0, n, place_suffix, 0)
    suffix_ref[...] = stage_ref[...].astype(jnp.bfloat16)
    absorb(suffix_ref, 0, tiles, False, True)
    for copy in w_copies:
        copy.wait_recv()
    for h in range(heads):
        rows = slice(h * SUF, (h + 1) * SUF)
        mixed = (acc_ref[rows, :] / sum_ref[rows, :1]).astype(jnp.bfloat16)
        out_ref[:, h * VHEAD:(h + 1) * VHEAD] = jnp.dot(
            mixed, wg_ref[:, h].reshape(VLAT, VHEAD), preferred_element_type=jnp.float32
        ).astype(jnp.bfloat16)
    for copy in started:
        copy.wait_send()


def fused(n, serve_n, tokens, block, w, queries, counts):
    depth = n // 4
    heads = queries.shape[1] // LAT
    dma = pltpu.SemaphoreType.DMA
    vmem = pl.BlockSpec(memory_space=pltpu.VMEM)
    return pl.pallas_call(
        functools.partial(fused_kernel, n, serve_n, tokens),
        out_shape=(
            jax.ShapeDtypeStruct((SUF, heads * VHEAD), jnp.bfloat16),
            jax.ShapeDtypeStruct((SUF, WIDE), jnp.bfloat16),
        ),
        in_specs=[vmem, vmem, vmem, pl.BlockSpec(memory_space=pltpu.SMEM)],
        out_specs=(vmem, vmem),
        scratch_shapes=[
            pltpu.VMEM((n,) + block.shape, jnp.bfloat16),
            pltpu.VMEM((serve_n,) + w.shape, jnp.bfloat16),
            pltpu.VMEM((heads * SUF, WIDE), jnp.bfloat16),
            pltpu.VMEM((4 * HOT * PAGE, WIDE), jnp.bfloat16),
            pltpu.VMEM((SUF, WIDE), jnp.float32),
            pltpu.VMEM((heads * SUF, VLAT), jnp.float32),
            pltpu.VMEM((heads * SUF, LANES), jnp.float32),
            pltpu.VMEM((heads * SUF, LANES), jnp.float32),
            dma((depth,)), dma((depth,)),
            dma((depth, 3)), dma((depth, 3)),
            dma((depth, 3)), dma((depth, 3)),
            dma((serve_n,)), dma((serve_n,)),
        ],
        compiler_params=pltpu.CompilerParams(
            collective_id=0, has_side_effects=True, vmem_limit_bytes=48 * 1024 * 1024
        ),
        name="fused",
    )(block, w, queries, counts)


def local(n, serve_n, queries, new_latent, pool, page_owner, page_slot, new_owner, new_slot,
          prefix_len, w_uv):
    holder = lax.axis_index("pool")
    owners = page_owner[0]
    slot_ids = page_slot[0]
    local_pages = pool[0]
    page_index = jnp.arange(PPAGES, dtype=jnp.int32)
    earlier = (page_index[None, :] < page_index[:, None]) & (owners[None, :] == owners[:, None])
    ranks = jnp.sum(earlier.astype(jnp.int32), axis=1)
    my_ranks = jnp.arange(HOT, dtype=jnp.int32)
    my_rows = (owners[None, :] == holder) & (ranks[None, :] == my_ranks[:, None])
    slot_rows = jnp.sum(jnp.where(my_rows, slot_ids[None, :], 0), axis=1)

    pages = local_pages[slot_rows].reshape(HOT, PAGE, LAT)
    latent = pages[:, :, :VLAT].reshape(HOT, PAGE, VLAT // LANES, LANES).transpose(0, 2, 1, 3)
    latent = latent.reshape(HOT, PAGE * VLAT // LANES, LANES)
    rope = pages[:, :, VLAT:].reshape(HOT, 2, PAGE // 2, ROPE).transpose(0, 2, 1, 3)
    rope = rope.reshape(HOT, PAGE // 2, LANES)
    packed = jnp.concatenate([latent, rope], axis=1).reshape(HOT * PAGE_ROWS, LANES)
    fresh = new_latent.reshape(-1, LAT)
    tokens = fresh.shape[0]
    fresh_latent = fresh[:, :VLAT].reshape(tokens, VLAT // LANES, LANES).transpose(1, 0, 2)
    fresh_rope = fresh[:, VLAT:].reshape(2, tokens // 2, ROPE).transpose(1, 0, 2)
    used = HOT * PAGE_ROWS + tokens * LAT // LANES
    block_rows = -(-used // 32) * 32
    filler = jnp.zeros((block_rows - used, LANES), jnp.bfloat16)
    block = jnp.concatenate(
        [packed, fresh_latent.reshape(-1, LANES), fresh_rope.reshape(-1, LANES), filler], axis=0
    )
    spots = jnp.arange(n * HOT, dtype=jnp.int32)
    held = jnp.clip(prefix_len[0] - PAGE * page_index, 0, PAGE)
    counts = jnp.sum(
        jnp.where(spots[:, None] == (owners * HOT + ranks)[None, :], held[None, :], 0), axis=1
    )
    attended, suffix = fused(n, serve_n, tokens, block, w_uv, queries[0], counts)
    fresh_pages = suffix[:, :LAT].reshape(NEWP, PAGE * LAT)
    placing = (jnp.arange(SLOTS, dtype=jnp.int32)[:, None] == new_slot[0][None, :]) & (
        new_owner[0][None, :] == holder
    )
    written = jnp.dot(
        placing.astype(jnp.bfloat16), fresh_pages, preferred_element_type=jnp.float32
    ).astype(jnp.bfloat16)
    updated = jnp.where(jnp.any(placing, axis=1)[:, None], written, local_pages)
    return (attended[None], updated[None])


def solution(mesh):
    in_specs = (
        P("serve", None, "pool"),
        P("serve", "pool"),
        P("serve", "pool", None),
        P("serve", None),
        P("serve", None),
        P("serve", None),
        P("serve", None),
        P("serve"),
        P("pool", "serve", None),
    )
    out_specs = (P("serve", None, "pool"), P("serve", "pool", None))
    body = functools.partial(local, mesh.shape["pool"], mesh.shape["serve"])
    return jax.shard_map(body, mesh=mesh, in_specs=in_specs, out_specs=out_specs, check_vma=False)
```

profile of v0, /device:TPU:18, one launch (start us, length us, event | category | flops | bytes accessed | tf_op | source)
XLA Modules:
  0.0 89.6 jit_solution(1256106764767035996)
XLA Ops:
  1.3 0.7 compare_bitcast_fusion
  2.0 0.7 compare_bitcast_fusion.1
  2.6 0.9 %convert_reduce_fusion = s32[32]{0:T(128)S(1)} fusion(s32[32]{0:T(128)} %bitcast.59), kind=kLoop, calls=%fused_computation.11 | loop fusion | flops 5088 | bytes 256 | tf_op jit(solution)/shard_map/reduce_sum | solution.py:285
  3.5 0.8 select_reduce_fusion.1
  4.3 0.7 fusion.10
  5.0 0.1 select_reduce_fusion.count_ref
  5.1 0.7 fusion.6
  5.8 0.1 pad.3.clone
  5.9 0.9 reduce
  6.8 0.1 reshape.69
  6.9 0.1 reshape.73
  7.0 0.0 copy-start
  7.0 2.5 %gather_fusion = bf16[3,36864]{1,0:T(4,128)(2,1)S(1)} fusion(bf16[12,36864]{1,0:T(8,128)(2,1)} %bitcast.49, s32[1024]{0:T(1024)S(1)} %pad_clamp_fusion), kind=kCustom, calls=%fused_computation | custom fusion | bytes 442380 | tf_op jit(solution)/shard_map/gather | solution.py:290
  9.6 0.0 copy-start.1
  9.6 0.3 reshape.63
  10.0 0.1 reshape.67
  10.1 0.2 maximum_maximum_fusion.block_ref
  10.3 0.0 copy-done
  10.3 0.3 copy-done.1
  10.6 0.0 copy-start.3
  10.6 73.1 %fused.1 = (bf16[256,1024]{1,0:T(8,128)(2,1)S(1)}, bf16[256,640]{1,0:T(8,128)(2,1)S(1)}) custom-call(bf16[960,128]{1,0:T(8,128)(2,1)S(1)} %maximum_maximum_fusion.block_ref, bf16[8,256,128]{2,1,0:T(8,128)(2,1)S(1)} %copy-done.1, bf16[256,4608]{1,0:T(8,128)(2,1)S(1)} %bitcast.46, s32[48]{0:T(128)S(1)} %select_reduce_fusion.count_ref), custom_call_target="tpu_custom_call" | custom-call | tf_op jit(solution)/shard_map/fused/pallas_call | solution.py:248
  83.7 0.0 copy-start.2
  83.7 0.7 copy-done.2
  84.4 1.4 %reshape.74 = bf16[4,36864]{1,0:T(4,128)(2,1)S(1)} reshape(bf16[256,576]{1,0:T(8,128)(2,1)} %bitcast.48) | data formatting | bytes 589824 | tf_op jit(solution)/shard_map/reshape | solution.py:312
  85.8 0.0 copy-done.3
  85.8 3.0 %fusion.1 = bf16[1,12,36864]{2,1,0:T(8,128)(2,1)} fusion(bf16[4,36864]{1,0:T(4,128)(2,1)S(1)} %reshape.74, pred[12]{0:T(512)(128)(4,1)S(1)} %fusion.6, s32[4]{0:T(128)S(1)} %bitcast.58, pred[4]{0:T(512)(128)(4,1)S(1)} %compare_bitcast_fusion, bf16[1,12,36864]{2,1,0:T(8,128)(2,1)} %param.11), kind=kOutput, calls=%fused_computation.3 | convolution fusion | flops 4423776 | bytes 2064416 | tf_op jit(solution)/shard_map/dot_general | solution.py:316
  88.8 0.8 copy.27
  (13 shorter events, 0.2 us)
Async XLA Ops:
  7.0 3.3 %copy-start = (bf16[1,256,4608]{2,1,0:T(8,128)(2,1)S(1)}, bf16[1,256,4608]{2,1,0:T(8,128)(2,1)}, u32[]{:S(2)}) copy-start(bf16[1,256,4608]{2,1,0:T(8,128)(2,1)} %param.9) | copy-start | bytes 7077892
  9.6 1.0 %copy-start.1 = (bf16[8,256,128]{2,1,0:T(8,128)(2,1)S(1)}, bf16[8,256,128]{2,1,0:T(8,128)(2,1)}, u32[]{:S(2)}) copy-start(bf16[8,256,128]{2,1,0:T(8,128)(2,1)} %w_ref.1) | copy-start | bytes 1572868
  10.6 75.2 %copy-start.3 = (s32[1,4]{1,0:T(1,128)S(1)}, s32[1,4]{1,0:T(1,128)}, u32[]{:S(2)}) copy-start(s32[1,4]{1,0:T(1,128)} %param.15) | copy-start | bytes 52
  83.7 0.7 copy-start.2
where the time goes:
time: 90.3 us; the launch traced here: 89.6 us
  Pallas kernels  73.1 us (81%)
  local copies, waits for them, and re-layouts  6.5 us (7%)
  other arithmetic  5.61 us (6%)
  matrix products  2.97 us (3%)
  between operations  1.43 us (2%)
    pallas_call x1, Pallas kernels, fused(): pl.pallas_call(functools.partial(fused_kernel, n, serve_n, tokens), out_s...  73.1 us
    dot_general x1, matrix products, local(): jnp.dot(placing.astype(jnp.bfloat16), fresh_pages, preferred_element_type...  2.97 us
    gather x1, local copies, waits for them, and re-layouts, local(): pages = local_pages[slot_rows].reshape(HOT, PAGE, LAT)  2.54 us

commit v1 on v0

v1 whole, which is shorter than its diff:
```python
import functools

import jax
import jax.numpy as jnp
from jax import lax
from jax.experimental import pallas as pl
from jax.experimental.pallas import tpu as pltpu
from jax.sharding import PartitionSpec as P

VLAT = 512
VHEAD = 128
PAGE = 64
SUF = 256
HOT = 3
LAT = 576
PPAGES = 32
NEWP = 4
SLOTS = 12

LANES = 128
ROPE = LAT - VLAT
WIDE = VLAT + LANES
PAIR = PAGE // 2
PAIR_ROWS = 2 * LAT // LANES
FLAT = PAGE * LAT // LANES
BLOCK = HOT * PAGE
SHELF = 16
TILE = 512
SUB = 256

softmax_scale = 192.0 ** (-0.5)
masked_score = -1e30
exp2_scale = softmax_scale * 1.4426950408889634

MESH = pl.DeviceIdType.MESH
contract_last = (((1,), (1,)), ((), ()))


def fused_kernel(n, serve_n, table_ref, owners_ref, raw_ref, pool_hbm, q_hbm, w_hbm, out_ref, new_ref,
                 pool_ref, poolf_ref, flat_ref, q_ref, w_ref, wg_ref, qs_ref, lat_ref, rope_ref,
                 kr_ref, raws_ref, rawf_ref, sfx_ref, count_ref, s_ref, acc_ref, top_ref, sum_ref,
                 local_sem, z_send, z_recv, x_send, x_recv, y_send, y_recv, w_send, w_recv,
                 r_send, r_recv):
    depth = n // 4
    heads = q_ref.shape[1] // LAT
    raw_rows = raw_ref.shape[0]
    me = lax.axis_index("pool")
    core = lax.axis_index("serve")
    x = me % 2
    y = (me // 2) % 2
    z = me // 4
    x_peer = z * 4 + y * 2 + (1 - x)
    y_peer = z * 4 + (1 - y) * 2 + x

    pool_copy = pltpu.make_async_copy(pool_hbm, pool_ref, local_sem.at[0])
    q_copy = pltpu.make_async_copy(q_hbm, q_ref, local_sem.at[1])
    w_copy = pltpu.make_async_copy(w_hbm, w_ref, local_sem.at[2])
    pool_copy.start()
    w_copy.start()
    q_copy.start()

    barrier = pltpu.get_barrier_semaphore()
    for p in range(1, n):
        pl.semaphore_signal(
            barrier, inc=1, device_id={"pool": (me + p) % n}, device_id_type=MESH
        )
    for d in range(1, serve_n):
        pl.semaphore_signal(
            barrier, inc=1, device_id={"serve": (core + d) % serve_n}, device_id_type=MESH
        )

    lane = lax.broadcasted_iota(jnp.int32, (PAIR, LANES), 1)

    rows = [jnp.int32(0)] * HOT
    seen = jnp.int32(0)
    for j in range(PPAGES):
        mine = table_ref[j] == me
        for r in range(HOT):
            rows[r] = jnp.where(mine & (seen == r), table_ref[PPAGES + j], rows[r])
        seen = seen + jnp.where(mine, 1, 0)

    pool_copy.wait()

    def widen(u, carry):
        for k in range(PAIR_ROWS):
            at = pl.multiple_of(u * PAIR_ROWS * LANES, LANES) + k * LANES
            to = pl.multiple_of(u * PAIR_ROWS * SHELF, SHELF) + k * SHELF
            poolf_ref[pl.ds(to, SLOTS), :] = pool_ref[:, pl.ds(at, LANES)].astype(jnp.float32)
        return carry

    lax.fori_loop(0, PAIR, widen, 0)

    def pick(u, carry):
        for r in range(HOT):
            for k in range(PAIR_ROWS):
                flat_ref[pl.ds(r * FLAT + u * PAIR_ROWS + k, 1), :] = poolf_ref[
                    pl.ds((u * PAIR_ROWS + k) * SHELF + rows[r], 1), :]
        return carry

    lax.fori_loop(0, PAIR, pick, 0)

    def halves(ref, start, count, lane):
        parts = [ref[pl.ds(start + k, count, stride=PAIR_ROWS), :] for k in range(PAIR_ROWS)]
        turned = [pltpu.roll(part, ROPE, 1) for part in parts[4:]]
        odd = [jnp.where(lane < ROPE, turned[c], turned[c + 1]) for c in range(4)]
        return parts, odd, turned[4]

    for r in range(HOT):
        parts, odd, _ = halves(flat_ref, r * FLAT, PAIR, lane)
        for c in range(4):
            at = slice(c * LANES, (c + 1) * LANES)
            lat_ref[0, 0, r * PAGE:r * PAGE + PAIR, at] = parts[c].astype(jnp.bfloat16)
            lat_ref[0, 0, r * PAGE + PAIR:(r + 1) * PAGE, at] = odd[c].astype(jnp.bfloat16)
        rope_ref[0, 0, r * PAIR:(r + 1) * PAIR, :] = jnp.where(
            lane < ROPE, parts[4], parts[8]).astype(jnp.bfloat16)

    owner_of = owners_ref[...]
    index = lax.broadcasted_iota(jnp.int32, (1, LANES), 1)
    held = jnp.clip(table_ref[2 * PPAGES + 2 * NEWP] - PAGE * index, 0, PAGE).astype(jnp.float32)
    named = owner_of == lax.broadcasted_iota(jnp.int32, (n, LANES), 0)
    before = (
        lax.broadcasted_iota(jnp.int32, (LANES, LANES), 0)
        < lax.broadcasted_iota(jnp.int32, (LANES, LANES), 1)
    )
    rank = jnp.dot(
        jnp.where(named, 1.0, 0.0).astype(jnp.bfloat16),
        jnp.where(before, 1.0, 0.0).astype(jnp.bfloat16),
        preferred_element_type=jnp.float32,
    )
    for r in range(HOT):
        count = jnp.sum(
            jnp.where(named & (rank == r), jnp.broadcast_to(held, (n, LANES)), 0.0),
            axis=1, keepdims=True,
        )
        count_ref[r] = jnp.broadcast_to(count, (n, LANES))

    raws_ref[pl.ds(me, 1)] = raw_ref[...][None]
    w_copy.wait()
    wg_ref[pl.ds(core, 1)] = w_ref[...][None]

    pl.semaphore_wait(barrier, n - 1 + serve_n - 1)

    started = []

    def send(src, dst, send_sem, recv_sem, device_id):
        copy = pltpu.make_async_remote_copy(
            src_ref=src, dst_ref=dst, send_sem=send_sem, recv_sem=recv_sem,
            device_id=device_id, device_id_type=MESH,
        )
        copy.start()
        started.append(copy)
        return copy

    order = []
    for d in range(1, depth // 2 + 1):
        order.append(d)
        if depth - d != d:
            order.append(depth - d)
    planes = [0] + order

    def base_of(d):
        return ((z - d + depth) % depth) * 4

    owners = {}
    for d in planes:
        base = base_of(d)
        owners[d, 0] = base + y * 2 + x
        owners[d, 1] = base + y * 2 + (1 - x)
        owners[d, 2] = base + (1 - y) * 2 + x
        owners[d, 3] = base + (1 - y) * 2 + (1 - x)

    def views(d, place, h):
        return (
            lat_ref.at[d, place, pl.ds(h * BLOCK // 2, BLOCK // 2)],
            rope_ref.at[d, place, pl.ds(h * BLOCK // 4, BLOCK // 4)],
        )

    arrivals = {}
    issued = {(0, 0)}

    def pass_on(src, dst, h, sends, recvs, d, slot, there):
        copies = []
        for part, (a, b) in enumerate(zip(views(*src, h), views(*dst, h))):
            copies.append(send(
                a, b, sends.at[d, slot, part], recvs.at[d, slot, part], {"pool": there}))
        arrivals[dst + (h,)] = copies
        issued.add(dst)

    def take(key):
        for copy in arrivals.pop(key, ()):
            copy.wait_recv()

    raw_copies = [
        send(raw_ref, raws_ref.at[me], r_send.at[p], r_recv.at[p], {"pool": (me + p) % n})
        for p in range(1, n)
    ]

    def spread(d, h):
        pass_on((d, 0), (d, 1), h, x_send, x_recv, d, h, x_peer)
        pass_on((d, 0), (d, 2), 1 - h, y_send, y_recv, d, 1 - h, y_peer)

    def forward(d):
        take((d, 1, 0))
        pass_on((d, 1), (d, 3), 0, y_send, y_recv, d, 2, y_peer)
        take((d, 2, 1))
        pass_on((d, 2), (d, 3), 1, x_send, x_recv, d, 2, x_peer)

    for h in range(2):
        spread(0, h)
    for d in order:
        there = ((z + d) % depth) * 4 + y * 2 + x
        for h in range(2):
            copies = []
            for part, (a, b) in enumerate(zip(views(0, 0, h), views(d, 0, h))):
                copies.append(send(
                    a, b, z_send.at[d, h, part], z_recv.at[d, h, part], {"pool": there}))
            arrivals[d, 0, h] = copies
            issued.add((d, 0))
    w_copies = [
        send(w_ref, wg_ref.at[core], w_send.at[d], w_recv.at[d], {"serve": (core + d) % serve_n})
        for d in range(1, serve_n)
    ]

    def advance(d):
        take((d, 0, 0))
        take((d, 0, 1))
        for h in range(2):
            spread(d, h)

    q_copy.wait()
    unit = jnp.where(
        lax.broadcasted_iota(jnp.int32, (SUF, WIDE - LAT), 1) == 0, 1.0, 0.0
    ).astype(jnp.bfloat16)
    for h in range(heads):
        qs_ref[h * SUF:(h + 1) * SUF, :] = jnp.concatenate(
            [q_ref[:, h * LAT:(h + 1) * LAT], unit], axis=1
        )

    def unpack(place, d, at):
        for r in range(HOT):
            rope = rope_ref[d, place, r * PAIR:(r + 1) * PAIR, :].astype(jnp.float32)
            count = count_ref[r, pl.ds(owners[d, place], 1), :]
            turned = pltpu.roll(rope, ROPE, 1)
            line = lax.broadcasted_iota(jnp.int32, (PAIR, LANES), 0).astype(jnp.float32)
            for k, values in enumerate((rope, turned)):
                absent = (lane == ROPE) & (2.0 * line + k >= count)
                tile = jnp.where(lane < ROPE, values, jnp.where(absent, masked_score, 0.0))
                kr_ref[at + r * PAGE + k * PAIR:at + r * PAGE + (k + 1) * PAIR, :] = tile.astype(
                    jnp.bfloat16)

    blocks = [(0, 0), (0, 1), (0, 2)]
    for k, d in enumerate(order):
        blocks += [(d, 0), (d, 1), (d, 2)]
        if k + 1 < len(order):
            blocks.append((planes[k], 3))
    blocks += [(planes[-2], 3), (planes[-1], 3)] if depth > 1 else [(0, 3)]
    pages = [(i, d, place, r) for i, (d, place) in enumerate(blocks) for r in range(HOT)]
    total = len(pages)
    cuts = [8]
    while total - cuts[-1] > 16:
        cuts.append(cuts[-1] + 12)
    cuts += [cuts[-1] + (total - cuts[-1]) // 2, total]
    chunks = [pages[a:b] for a, b in zip([0] + cuts[:-1], cuts)]

    tiles = heads * SUF // TILE

    def loader(chunk):
        def latents(first, count):
            return jnp.concatenate(
                [lat_ref[d, place, r * PAGE:(r + 1) * PAGE, :]
                 for _, d, place, r in chunk[first // PAGE:(first + count) // PAGE]], axis=0)

        def keys(first, count):
            at = (chunk[0][0] * HOT + chunk[0][3]) * PAGE + first
            return jnp.concatenate([latents(first, count), kr_ref[at:at + count, :]], axis=1)

        return latents, keys, len(chunk) * PAGE

    def suffix_loader():
        return (
            lambda first, count: sfx_ref[first:first + count, :VLAT],
            lambda first, count: sfx_ref[first:first + count, :],
            SUF,
        )

    def score(t, load, slot):
        _, keys, size = load
        for at in range(0, size, SUB):
            s_ref[slot, :, at:at + SUB] = lax.dot_general(
                qs_ref[t * TILE:(t + 1) * TILE, :], keys(at, SUB), contract_last,
                preferred_element_type=jnp.float32,
            )

    def absorb(t, load, slot, first, causal):
        latents, _, size = load
        rows = slice(t * TILE, (t + 1) * TILE)
        strips = [s_ref[slot, :, c * LANES:(c + 1) * LANES] for c in range(size // LANES)]
        if causal:
            row = lax.broadcasted_iota(jnp.int32, (TILE, LANES), 0) % SUF
            col = lax.broadcasted_iota(jnp.int32, (TILE, LANES), 1)
            for c in range(size // LANES):
                token = c * LANES + col
                token = jnp.where(token < SUF // 2, 2 * token, 2 * token - SUF + 1)
                strips[c] = jnp.where(token <= row, strips[c], masked_score)
        top = strips[0]
        for strip in strips[1:]:
            top = jnp.maximum(top, strip)
        top = jnp.broadcast_to(jnp.max(top, axis=1, keepdims=True), (TILE, LANES))
        if not first:
            earlier = top_ref[rows, :]
            top = jnp.maximum(top, earlier)
        shift = top * exp2_scale
        weights = []
        added = None
        for strip in strips:
            weight = jnp.exp2(strip * exp2_scale - shift)
            added = weight if added is None else added + weight
            weights.append(weight.astype(jnp.bfloat16))
        mixed = jnp.dot(
            jnp.concatenate(weights, axis=1), latents(0, size), preferred_element_type=jnp.float32
        )
        if not first:
            rescale = jnp.exp2((earlier - top) * exp2_scale)
            added = added + sum_ref[rows, :] * rescale
            mixed = mixed + acc_ref[rows, :] * jnp.concatenate([rescale] * (VLAT // LANES), axis=1)
        top_ref[rows, :] = top
        sum_ref[rows, :] = added
        acc_ref[rows, :] = mixed

    def attend(load, first, causal, between):
        score(0, load, 0)
        for t in range(tiles):
            if t + 1 < tiles:
                score(t + 1, load, (t + 1) % 2)
            absorb(t, load, t % 2, first, causal)
            between(t)

    pending = []
    for k, d in enumerate(planes):
        pending.append(functools.partial(forward, d))
        if k + 1 < depth:
            pending.append(functools.partial(advance, planes[k + 1]))

    def communicate(steps):
        for _ in range(min(steps, len(pending))):
            pending.pop(0)()

    for copy in raw_copies:
        copy.wait_recv()
    for o in range(n):
        rawf_ref[o * raw_rows:(o + 1) * raw_rows, :] = raws_ref[o].astype(jnp.float32)
    wide_lane = lax.broadcasted_iota(jnp.int32, (SUF // 2, LANES), 1)
    parts, odd, last = halves(rawf_ref, 0, SUF // 2, wide_lane)
    for c in range(4):
        at = slice(c * LANES, (c + 1) * LANES)
        sfx_ref[:SUF // 2, at] = parts[c].astype(jnp.bfloat16)
        sfx_ref[SUF // 2:, at] = odd[c].astype(jnp.bfloat16)
    for half, values in enumerate((parts[4], last)):
        sfx_ref[half * SUF // 2:(half + 1) * SUF // 2, VLAT:] = jnp.where(
            wide_lane < ROPE, values, 0.0).astype(jnp.bfloat16)

    attend(suffix_loader(), True, True, lambda t: None)
    communicate(1)

    page = jnp.int32(0)
    slot = jnp.int32(-1)
    for m in range(NEWP):
        mine = table_ref[2 * PPAGES + m] == me
        page = jnp.where(mine, m, page)
        slot = jnp.where(mine, table_ref[2 * PPAGES + NEWP + m], slot)
    chosen = lax.broadcasted_iota(jnp.int32, (SLOTS, LANES), 0) == slot

    def write(u, carry):
        for k in range(PAIR_ROWS):
            at = pl.multiple_of(u * PAIR_ROWS * LANES, LANES) + k * LANES
            fresh = rawf_ref[pl.ds(page * FLAT + u * PAIR_ROWS + k, 1), :]
            to = pl.multiple_of(u * PAIR_ROWS * SHELF, SHELF) + k * SHELF
            kept = poolf_ref[pl.ds(to, SLOTS), :]
            new_ref[:, pl.ds(at, LANES)] = jnp.where(chosen, fresh, kept).astype(jnp.bfloat16)
        return carry

    lax.fori_loop(0, PAIR, write, 0)

    ready = 0
    for k, chunk in enumerate(chunks):
        while ready <= chunk[-1][0]:
            d, place = blocks[ready]
            while (d, place) not in issued:
                communicate(1)
            take((d, place, 0))
            take((d, place, 1))
            unpack(place, d, ready * BLOCK)
            ready += 1
        attend(loader(chunk), False, False, lambda t: communicate(1) if t % 2 else None)
    for copy in w_copies:
        copy.wait_recv()
    for h in range(heads):
        rows = slice(h * SUF, (h + 1) * SUF)
        mixed = (acc_ref[rows, :] / jnp.sum(sum_ref[rows, :], axis=1, keepdims=True)).astype(
            jnp.bfloat16)
        out_ref[:, h * VHEAD:(h + 1) * VHEAD] = jnp.dot(
            mixed, wg_ref[:, h].reshape(VLAT, VHEAD), preferred_element_type=jnp.float32
        ).astype(jnp.bfloat16)
    for copy in started:
        copy.wait_send()


def fused(n, serve_n, table, owners, raw, pages, queries, w):
    depth = n // 4
    heads = queries.shape[1] // LAT
    dma = pltpu.SemaphoreType.DMA
    vmem = pl.BlockSpec(memory_space=pltpu.VMEM)
    hbm = pl.BlockSpec(memory_space=pl.ANY)
    bf16, f32 = jnp.bfloat16, jnp.float32
    rows = heads * SUF
    return pl.pallas_call(
        functools.partial(fused_kernel, n, serve_n),
        out_shape=(
            jax.ShapeDtypeStruct((SUF, heads * VHEAD), bf16),
            jax.ShapeDtypeStruct(pages.shape, bf16),
        ),
        in_specs=[pl.BlockSpec(memory_space=pltpu.SMEM), vmem, vmem, hbm, hbm, hbm],
        out_specs=(vmem, vmem),
        scratch_shapes=[
            pltpu.VMEM(pages.shape, bf16),
            pltpu.VMEM((FLAT * SHELF, LANES), f32),
            pltpu.VMEM((HOT * FLAT, LANES), f32),
            pltpu.VMEM(queries.shape, bf16),
            pltpu.VMEM(w.shape, bf16),
            pltpu.VMEM((serve_n,) + w.shape, bf16),
            pltpu.VMEM((rows, WIDE), bf16),
            pltpu.VMEM((depth, 4, BLOCK, VLAT), bf16),
            pltpu.VMEM((depth, 4, BLOCK // 2, LANES), bf16),
            pltpu.VMEM((n * BLOCK, LANES), bf16),
            pltpu.VMEM((n,) + raw.shape, bf16),
            pltpu.VMEM((n * raw.shape[0], LANES), f32),
            pltpu.VMEM((SUF, WIDE), bf16),
            pltpu.VMEM((HOT, n, LANES), f32),
            pltpu.VMEM((2, TILE, 12 * PAGE), f32),
            pltpu.VMEM((rows, VLAT), f32),
            pltpu.VMEM((rows, LANES), f32),
            pltpu.VMEM((rows, LANES), f32),
            dma((3,)),
            dma((depth, 2, 2)), dma((depth, 2, 2)),
            dma((depth, 3, 2)), dma((depth, 3, 2)),
            dma((depth, 3, 2)), dma((depth, 3, 2)),
            dma((serve_n,)), dma((serve_n,)),
            dma((n,)), dma((n,)),
        ],
        compiler_params=pltpu.CompilerParams(
            collective_id=0, has_side_effects=True, vmem_limit_bytes=56 * 1024 * 1024
        ),
        name="fused",
    )(table, owners, raw, pages, queries, w)


def local(n, serve_n, queries, new_latent, pool, page_owner, page_slot, new_owner, new_slot,
          prefix_len, w_uv):
    table = jnp.concatenate([page_owner[0], page_slot[0], new_owner[0], new_slot[0], prefix_len])
    owners = jnp.pad(page_owner, ((0, 0), (0, LANES - PPAGES)), constant_values=-1)
    raw = new_latent.reshape(-1, LANES)
    attended, updated = fused(n, serve_n, table, owners, raw, pool[0], queries[0], w_uv)
    return (attended[None], updated[None])


def solution(mesh):
    in_specs = (
        P("serve", None, "pool"),
        P("serve", "pool"),
        P("serve", "pool", None),
        P("serve", None),
        P("serve", None),
        P("serve", None),
        P("serve", None),
        P("serve"),
        P("pool", "serve", None),
    )
    out_specs = (P("serve", None, "pool"), P("serve", "pool", None))
    body = functools.partial(local, mesh.shape["pool"], mesh.shape["serve"])
    return jax.shard_map(body, mesh=mesh, in_specs=in_specs, out_specs=out_specs, check_vma=False)
```

time: 90.3 us -> 70.2 us (0.78)
  Pallas kernels: 73.1 us -> 60.3 us
  other arithmetic: 5.61 us -> 1.47 us
  matrix products: 2.97 us -> 0 us
    pallas_call x1, Pallas kernels: 73.1 us -> 60.3 us  [fused(): pl.pallas_call(functools.partial(fused_kernel, n, serve_n), out_shape=(ja...]
    dot_general x1 -> x0, matrix products: 2.97 us -> none  [local(): jnp.dot(placing.astype(jnp.bfloat16), fresh_pages, preferred_element_type...]
    gather x1 -> x0, local copies, waits for them, and re-layouts: 2.54 us -> none  [local(): pages = local_pages[slot_rows].reshape(HOT, PAGE, LAT)]
    unnamed x9 -> x2, local copies, waits for them, and re-layouts: 1.8 us -> 4.23 us
    reshape x8 -> x0, local copies, waits for them, and re-layouts: 2.04 us -> none  [the longest x1 1.37 us: local(): fresh_pages = suffix[:, :LAT].reshape(NEWP, PAGE * LAT)]
    reduce_sum x3 -> x0, other arithmetic: 1.78 us -> none  [the longest x1 0.91 us: local(): ranks = jnp.sum(earlier.astype(jnp.int32), axis=1)]
    and x2 -> x0, other arithmetic: 1.32 us -> none  [the longest x1 0.66 us: local(): (jnp.arange(SLOTS, dtype=jnp.int32)[:, None] == new_slot[0][None, :]) & (...]
    concatenate x1, local copies, waits for them, and re-layouts: 0.08 us -> 1.3 us  [local(): jnp.concatenate([page_owner[0], page_slot[0], new_owner[0], new_slot[0],...]
where the time goes in v1:
time: 70.2 us; the launch traced here: 69.8 us
  Pallas kernels  60.3 us (86%)
  local copies, waits for them, and re-layouts  6.72 us (10%)
  other arithmetic  1.47 us (2%)
  between operations  1.29 us (2%)
    pallas_call x1, Pallas kernels, fused(): pl.pallas_call(functools.partial(fused_kernel, n, serve_n), out_shape=(ja...  60.3 us
    unnamed x2, local copies, waits for them, and re-layouts  4.23 us
    unnamed x1, other arithmetic  1.47 us

profile of v1, /device:TPU:18, one launch (start us, length us, event | category | flops | bytes accessed | tf_op | source)
XLA Modules:
  0.0 69.8 jit_solution(1262555403078422856)
XLA Ops:
  1.3 1.3 %concatenate.3.table_ref = s32[73]{0:T(128)} concatenate(s32[32]{0:T(128)} %bitcast.17, s32[32]{0:T(128)} %bitcast.14, s32[4]{0:T(128)} %bitcast.15, s32[4]{0:T(128)} %bitcast.16, s32[1]{0:T(128)S(6)} %copy.13), dimensions={0} | concatenate | bytes 584 | tf_op jit(solution)/shard_map/concatenate | solution.py:459
  2.6 1.2 %pad.4.owners_ref = s32[1,128]{1,0:T(1,128)} pad(s32[1,32]{1,0:T(1,128)} %param.12, s32[]{:T(128)} %constant.0.clone.1), padding=0_0x0_96 | pad | bytes 644 | tf_op jit(solution)/shard_map/jit(_pad)/pad | solution.py:460
  3.8 1.5 %reduce = bf16[9216]{0:T(1024)(128)(2,1)} reduce(bf16[1,9216]{1,0:T(2,128)(2,1)} %param.10, bf16[]{:T(256)} %constant.13), dimensions={0}, to_apply=%param.10.reduce_sub_computation | reduce | bytes 36866 | tf_op args[1]
  5.2 60.3 %fused.1 = (bf16[256,1024]{1,0:T(8,128)(2,1)}, bf16[12,36864]{1,0:T(8,128)(2,1)}) custom-call(s32[73]{0:T(128)} %concatenate.3.table_ref, s32[1,128]{1,0:T(1,128)} %pad.4.owners_ref, bf16[72,128]{1,0:T(8,128)(2,1)} %bitcast.13, bf16[12,36864]{1,0:T(8,128)(2,1)} %bitcast.11, bf16[256,4608]{1,0:T(8,128)(2,1)} %bitcast.9, bf16[8,256,128]{2,1,0:T(8,128)(2,1)} %w_hbm.1), custom_call_target="tpu_custom_call" | custom-call | tf_op jit(solution)/shard_map/fused/pallas_call | solution.py:416
  65.6 1.9 %copy.14 = bf16[1,256,1024]{2,1,0:T(8,128)(2,1)} copy(bf16[1,256,1024]{2,1,0:T(8,128)(2,1)} %bitcast.12) | data formatting | bytes 1048576
  67.5 2.4 %copy.15 = bf16[1,12,36864]{2,1,0:T(8,128)(2,1)} copy(bf16[1,12,36864]{2,1,0:T(8,128)(2,1)} %bitcast.10) | data formatting | bytes 1769472

commit v2 on v1

v2 whole, which is shorter than its diff:
```python
import functools

import jax
import jax.numpy as jnp
from jax import lax
from jax.experimental import pallas as pl
from jax.experimental.pallas import tpu as pltpu
from jax.sharding import PartitionSpec as P

VLAT = 512
VHEAD = 128
PAGE = 64
SUF = 256
HOT = 3
LAT = 576
PPAGES = 32
NEWP = 4
SLOTS = 12

LANES = 128
ROPE = LAT - VLAT
WIDE = VLAT + LANES
PAIR = PAGE // 2
PAIR_ROWS = 2 * LAT // LANES
FLAT = PAGE * LAT // LANES
BLOCK = HOT * PAGE
SHELF = 16
TILE = 512
SUB = 256

softmax_scale = 192.0 ** (-0.5)
masked_score = -1e30
exp2_scale = softmax_scale * 1.4426950408889634

MESH = pl.DeviceIdType.MESH
contract_last = (((1,), (1,)), ((), ()))


def fused_kernel(n, serve_n, owner_hbm, slot_hbm, new_owner_hbm, new_slot_hbm, len_ref, fresh_hbm,
                 pool_hbm, q_hbm, w_hbm, out_ref, new_ref,
                 owner_ref, slot_ref, new_owner_ref, new_slot_ref, named_ref, fresh_ref,
                 pool_ref, poolf_ref, flat_ref, own_ref, raw_ref, q_ref, w_ref, wg_ref, qs_ref,
                 lat_ref, rope_ref, kr_ref, raws_ref, rawf_ref, sfx_ref, count_ref, s_ref, acc_ref,
                 top_ref, sum_ref, local_sem, z_send, z_recv, x_send, x_recv, y_send, y_recv,
                 c_send, w_send, w_recv, rz_send, rz_recv, r_send, r_recv):
    depth = n // 4
    heads = q_ref.shape[1] // LAT
    raw_rows = raw_ref.shape[0]
    me = lax.axis_index("pool")
    core = lax.axis_index("serve")
    x = me % 2
    y = (me // 2) % 2
    z = me // 4
    x_peer = z * 4 + y * 2 + (1 - x)
    y_peer = z * 4 + (1 - y) * 2 + x
    far_peer = z * 4 + (1 - y) * 2 + (1 - x)
    column = [((z + d) % depth) * 4 + y * 2 + x for d in range(depth)]

    fetches = [
        pltpu.make_async_copy(src, dst, local_sem.at[i])
        for i, (src, dst) in enumerate((
            (owner_hbm, owner_ref), (slot_hbm, slot_ref), (pool_hbm, pool_ref),
            (fresh_hbm, fresh_ref), (w_hbm, w_ref), (q_hbm, q_ref), (owner_hbm, named_ref),
            (new_owner_hbm, new_owner_ref), (new_slot_hbm, new_slot_ref),
        ))
    ]
    for fetch in fetches:
        fetch.start()

    barrier = pltpu.get_barrier_semaphore()
    peers = column[1:] + [x_peer, y_peer, far_peer]
    for there in peers:
        pl.semaphore_signal(barrier, inc=1, device_id={"pool": there}, device_id_type=MESH)
    for d in range(1, serve_n):
        pl.semaphore_signal(
            barrier, inc=1, device_id={"serve": (core + d) % serve_n}, device_id_type=MESH
        )

    lane = lax.broadcasted_iota(jnp.int32, (PAIR, LANES), 1)

    fetches[0].wait()
    fetches[1].wait()
    rows = [jnp.int32(0)] * HOT
    seen = jnp.int32(0)
    for j in range(PPAGES):
        mine = owner_ref[0, j] == me
        for r in range(HOT):
            rows[r] = jnp.where(mine & (seen == r), slot_ref[0, j], rows[r])
        seen = seen + jnp.where(mine, 1, 0)

    fetches[2].wait()

    def widen(u, carry):
        for k in range(PAIR_ROWS):
            at = pl.multiple_of(u * PAIR_ROWS * LANES, LANES) + k * LANES
            to = pl.multiple_of(u * PAIR_ROWS * SHELF, SHELF) + k * SHELF
            poolf_ref[pl.ds(to, SLOTS), :] = pool_ref[:, pl.ds(at, LANES)].astype(jnp.float32)
        return carry

    lax.fori_loop(0, PAIR, widen, 0)

    def pick(u, carry):
        for r in range(HOT):
            for k in range(PAIR_ROWS):
                flat_ref[pl.ds(r * FLAT + u * PAIR_ROWS + k, 1), :] = poolf_ref[
                    pl.ds((u * PAIR_ROWS + k) * SHELF + rows[r], 1), :]
        return carry

    lax.fori_loop(0, PAIR, pick, 0)

    def halves(ref, start, count, lane):
        parts = [ref[pl.ds(start + k, count, stride=PAIR_ROWS), :] for k in range(PAIR_ROWS)]
        turned = [pltpu.roll(part, ROPE, 1) for part in parts[4:]]
        odd = [jnp.where(lane < ROPE, turned[c], turned[c + 1]) for c in range(4)]
        return parts, odd, turned[4]

    for r in range(HOT):
        parts, odd, _ = halves(flat_ref, r * FLAT, PAIR, lane)
        for c in range(4):
            at = slice(c * LANES, (c + 1) * LANES)
            lat_ref[0, 0, r * PAGE:r * PAGE + PAIR, at] = parts[c].astype(jnp.bfloat16)
            lat_ref[0, 0, r * PAGE + PAIR:(r + 1) * PAGE, at] = odd[c].astype(jnp.bfloat16)
        rope_ref[0, 0, r * PAIR:(r + 1) * PAIR, :] = jnp.where(
            lane < ROPE, parts[4], parts[8]).astype(jnp.bfloat16)

    fetches[3].wait()
    for k in range(raw_rows):
        own_ref[k:k + 1, :] = fresh_ref[:, k * LANES:(k + 1) * LANES].astype(jnp.float32)
    raw_ref[...] = own_ref[...].astype(jnp.bfloat16)
    fetches[4].wait()

    pl.semaphore_wait(barrier, len(peers) + serve_n - 1)

    started = []

    def send(src, dst, send_sem, recv_sem, device_id):
        copy = pltpu.make_async_remote_copy(
            src_ref=src, dst_ref=dst, send_sem=send_sem, recv_sem=recv_sem,
            device_id=device_id, device_id_type=MESH,
        )
        copy.start()
        started.append(copy)
        return copy

    order = []
    for d in range(1, depth // 2 + 1):
        order.append(d)
        if depth - d != d:
            order.append(depth - d)
    planes = [0] + order

    def base_of(d):
        return ((z - d + depth) % depth) * 4

    owners = {}
    for d in planes:
        base = base_of(d)
        owners[d, 0] = base + y * 2 + x
        owners[d, 1] = base + y * 2 + (1 - x)
        owners[d, 2] = base + (1 - y) * 2 + x
        owners[d, 3] = base + (1 - y) * 2 + (1 - x)

    def views(d, place, h):
        return (
            lat_ref.at[d, place, pl.ds(h * BLOCK // 2, BLOCK // 2)],
            rope_ref.at[d, place, pl.ds(h * BLOCK // 4, BLOCK // 4)],
        )

    arrivals = {}
    issued = {(0, 0)}

    def pass_on(src, dst, h, sends, recvs, d, slot, there):
        copies = []
        for part, (a, b) in enumerate(zip(views(*src, h), views(*dst, h))):
            copies.append(send(
                a, b, sends.at[d, slot, part], recvs.at[d, slot, part], {"pool": there}))
        arrivals[dst + (h,)] = copies
        issued.add(dst)

    def take(key):
        for copy in arrivals.pop(key, ()):
            copy.wait_recv()

    def spread(d, h):
        pass_on((d, 0), (d, 1), h, x_send, x_recv, d, h, x_peer)
        pass_on((d, 0), (d, 2), 1 - h, y_send, y_recv, d, 1 - h, y_peer)

    def start_if(condition, copies):
        @pl.when(condition)
        def _():
            for copy in copies:
                copy.start()
        guarded.append((condition, copies))

    def halved(src, dst, there, sends, recvs):
        return [
            pltpu.make_async_remote_copy(
                src_ref=a, dst_ref=b, send_sem=sends.at[part], recv_sem=recvs.at[part],
                device_id={"pool": there}, device_id_type=MESH,
            )
            for part, (a, b) in enumerate(zip(src, dst))
        ]

    guarded = []
    near = {1: (z == 0, z < depth - 1), depth - 1: (z == depth - 1, z > 0)}

    def forward(d):
        for place, h, there, sends, recvs in (
            (1, 0, y_peer, y_send, y_recv), (2, 1, x_peer, x_send, x_recv)
        ):
            take((d, place, h))
            if d in near:
                copies = halved(views(d, place, h), views(d, 3, h), there,
                                sends.at[d, 2], recvs.at[d, 2])
                start_if(near[d][0], copies)
                arrivals[d, 3, h] = copies
                issued.add((d, 3))
            else:
                pass_on((d, place), (d, 3), h, sends, recvs, d, 2, there)

    def cross():
        for h, recvs in ((0, y_recv), (1, x_recv)):
            take((0, 3, h))
        for i, d in enumerate(near):
            copies = []
            for h, recvs in ((0, y_recv), (1, x_recv)):
                copies += halved(views(0, 3, h), views(d, 3, h), column[d],
                                 c_send.at[i, h], recvs.at[d, 2])
            start_if(near[d][1], copies)

    raw_column = {
        d: send(raw_ref, raws_ref.at[me], rz_send.at[d], rz_recv.at[d], {"pool": column[d]})
        for d in order
    }
    for h in range(2):
        spread(0, h)
    for d in order:
        for h in range(2):
            copies = []
            for part, (a, b) in enumerate(zip(views(0, 0, h), views(d, 0, h))):
                copies.append(send(
                    a, b, z_send.at[d, h, part], z_recv.at[d, h, part], {"pool": column[d]}))
            arrivals[d, 0, h] = copies
            issued.add((d, 0))

    raw_copies = []

    def pass_raw(d):
        owner = owners[d, 0]
        src = raw_ref if d == 0 else raws_ref.at[owner]
        for i, there in enumerate((x_peer, y_peer, far_peer)):
            raw_copies.append(send(
                src, raws_ref.at[owner], r_send.at[d, i], r_recv.at[d, i], {"pool": there}))

    pass_raw(0)
    w_copies = [
        send(w_ref, wg_ref.at[core], w_send.at[d], w_recv.at[d], {"serve": (core + d) % serve_n})
        for d in range(1, serve_n)
    ]

    def advance(d):
        take((d, 0, 0))
        take((d, 0, 1))
        for h in range(2):
            spread(d, h)

    for fetch in fetches[6:]:
        fetch.wait()
    index = lax.broadcasted_iota(jnp.int32, (1, PPAGES), 1)
    held = jnp.clip(len_ref[0] - PAGE * index, 0, PAGE).astype(jnp.float32)
    named = named_ref[...] == lax.broadcasted_iota(jnp.int32, (n, PPAGES), 0)
    before = (
        lax.broadcasted_iota(jnp.int32, (PPAGES, PPAGES), 0)
        < lax.broadcasted_iota(jnp.int32, (PPAGES, PPAGES), 1)
    )
    rank = jnp.dot(
        jnp.where(named, 1.0, 0.0).astype(jnp.bfloat16),
        jnp.where(before, 1.0, 0.0).astype(jnp.bfloat16),
        preferred_element_type=jnp.float32,
    )
    for r in range(HOT):
        count = jnp.sum(
            jnp.where(named & (rank == r), jnp.broadcast_to(held, (n, PPAGES)), 0.0),
            axis=1, keepdims=True,
        )
        count_ref[r] = jnp.broadcast_to(count, (n, LANES))

    raws_ref[pl.ds(me, 1)] = raw_ref[...][None]
    wg_ref[pl.ds(core, 1)] = w_ref[...][None]
    fetches[5].wait()
    unit = jnp.where(
        lax.broadcasted_iota(jnp.int32, (SUF, WIDE - LAT), 1) == 0, 1.0, 0.0
    ).astype(jnp.bfloat16)
    for h in range(heads):
        qs_ref[h * SUF:(h + 1) * SUF, :] = jnp.concatenate(
            [q_ref[:, h * LAT:(h + 1) * LAT], unit], axis=1
        )

    def unpack(place, d, at):
        for r in range(HOT):
            rope = rope_ref[d, place, r * PAIR:(r + 1) * PAIR, :].astype(jnp.float32)
            count = count_ref[r, pl.ds(owners[d, place], 1), :]
            turned = pltpu.roll(rope, ROPE, 1)
            line = lax.broadcasted_iota(jnp.int32, (PAIR, LANES), 0).astype(jnp.float32)
            for k, values in enumerate((rope, turned)):
                absent = (lane == ROPE) & (2.0 * line + k >= count)
                tile = jnp.where(lane < ROPE, values, jnp.where(absent, masked_score, 0.0))
                kr_ref[at + r * PAGE + k * PAIR:at + r * PAGE + (k + 1) * PAIR, :] = tile.astype(
                    jnp.bfloat16)

    for d in order:
        raw_column[d].wait_recv()
        pass_raw(d)

    blocks = [(0, 0), (0, 1), (0, 2)]
    for k, d in enumerate(order):
        blocks += [(d, 0), (d, 1), (d, 2)]
        if k == 0:
            blocks.append((0, 3))
    blocks += [(d, 3) for d in order]
    pages = [(i, d, place, r) for i, (d, place) in enumerate(blocks) for r in range(HOT)]
    total = len(pages)
    cuts = [8]
    while total - cuts[-1] > 16:
        cuts.append(cuts[-1] + 12)
    cuts += [cuts[-1] + (total - cuts[-1]) // 2, total]
    chunks = [pages[a:b] for a, b in zip([0] + cuts[:-1], cuts)]

    tiles = heads * SUF // TILE

    def loader(chunk):
        def latents(first, count):
            return jnp.concatenate(
                [lat_ref[d, place, r * PAGE:(r + 1) * PAGE, :]
                 for _, d, place, r in chunk[first // PAGE:(first + count) // PAGE]], axis=0)

        def keys(first, count):
            at = (chunk[0][0] * HOT + chunk[0][3]) * PAGE + first
            return jnp.concatenate([latents(first, count), kr_ref[at:at + count, :]], axis=1)

        return latents, keys, len(chunk) * PAGE

    def suffix_loader():
        return (
            lambda first, count: sfx_ref[first:first + count, :VLAT],
            lambda first, count: sfx_ref[first:first + count, :],
            SUF,
        )

    def score(t, load, slot):
        _, keys, size = load
        for at in range(0, size, SUB):
            s_ref[slot, :, at:at + SUB] = lax.dot_general(
                qs_ref[t * TILE:(t + 1) * TILE, :], keys(at, SUB), contract_last,
                preferred_element_type=jnp.float32,
            )

    def absorb(t, load, slot, first, causal):
        latents, _, size = load
        rows = slice(t * TILE, (t + 1) * TILE)
        strips = [s_ref[slot, :, c * LANES:(c + 1) * LANES] for c in range(size // LANES)]
        if causal:
            row = lax.broadcasted_iota(jnp.int32, (TILE, LANES), 0) % SUF
            col = lax.broadcasted_iota(jnp.int32, (TILE, LANES), 1)
            for c in range(size // LANES):
                token = c * LANES + col
                token = jnp.where(token < SUF // 2, 2 * token, 2 * token - SUF + 1)
                strips[c] = jnp.where(token <= row, strips[c], masked_score)
        top = strips[0]
        for strip in strips[1:]:
            top = jnp.maximum(top, strip)
        top = jnp.broadcast_to(jnp.max(top, axis=1, keepdims=True), (TILE, LANES))
        if not first:
            earlier = top_ref[rows, :]
            top = jnp.maximum(top, earlier)
        shift = top * exp2_scale
        weights = []
        added = None
        for strip in strips:
            weight = jnp.exp2(strip * exp2_scale - shift)
            added = weight if added is None else added + weight
            weights.append(weight.astype(jnp.bfloat16))
        mixed = jnp.dot(
            jnp.concatenate(weights, axis=1), latents(0, size), preferred_element_type=jnp.float32
        )
        if not first:
            rescale = jnp.exp2((earlier - top) * exp2_scale)
            added = added + sum_ref[rows, :] * rescale
            mixed = mixed + acc_ref[rows, :] * jnp.concatenate([rescale] * (VLAT // LANES), axis=1)
        top_ref[rows, :] = top
        sum_ref[rows, :] = added
        acc_ref[rows, :] = mixed

    def attend(load, first, causal, between):
        score(0, load, 0)
        for t in range(tiles):
            if t + 1 < tiles:
                score(t + 1, load, (t + 1) % 2)
            absorb(t, load, t % 2, first, causal)
            between(t)

    pending = [functools.partial(forward, 0)]
    for k, d in enumerate(order):
        pending.append(functools.partial(advance, d))
        if k == 0:
            pending.append(cross)
        pending.append(functools.partial(forward, d))

    def communicate(steps):
        for _ in range(min(steps, len(pending))):
            pending.pop(0)()

    def suffix():
        for copy in raw_copies:
            copy.wait_recv()
        for o in range(n):
            rawf_ref[o * raw_rows:(o + 1) * raw_rows, :] = raws_ref[o].astype(jnp.float32)
        wide_lane = lax.broadcasted_iota(jnp.int32, (SUF // 2, LANES), 1)
        parts, odd, last = halves(rawf_ref, 0, SUF // 2, wide_lane)
        for c in range(4):
            at = slice(c * LANES, (c + 1) * LANES)
            sfx_ref[:SUF // 2, at] = parts[c].astype(jnp.bfloat16)
            sfx_ref[SUF // 2:, at] = odd[c].astype(jnp.bfloat16)
        for half, values in enumerate((parts[4], last)):
            sfx_ref[half * SUF // 2:(half + 1) * SUF // 2, VLAT:] = jnp.where(
                wide_lane < ROPE, values, 0.0).astype(jnp.bfloat16)

        attend(suffix_loader(), False, True, lambda t: communicate(1) if t % 2 else None)

        page = jnp.int32(0)
        slot = jnp.int32(-1)
        for m in range(NEWP):
            mine = new_owner_ref[0, m] == me
            page = jnp.where(mine, m, page)
            slot = jnp.where(mine, new_slot_ref[0, m], slot)
        chosen = lax.broadcasted_iota(jnp.int32, (SLOTS, LANES), 0) == slot

        def write(u, carry):
            for k in range(PAIR_ROWS):
                at = pl.multiple_of(u * PAIR_ROWS * LANES, LANES) + k * LANES
                fresh = rawf_ref[pl.ds(page * FLAT + u * PAIR_ROWS + k, 1), :]
                to = pl.multiple_of(u * PAIR_ROWS * SHELF, SHELF) + k * SHELF
                kept = poolf_ref[pl.ds(to, SLOTS), :]
                new_ref[:, pl.ds(at, LANES)] = jnp.where(chosen, fresh, kept).astype(jnp.bfloat16)
            return carry

        lax.fori_loop(0, PAIR, write, 0)

    steps = [{0: 1, 2: 1}, {3: 1}, {0: 1, 3: 1}]

    communicate(1)
    ready = 0
    for k, chunk in enumerate(chunks):
        while ready <= chunk[-1][0]:
            d, place = blocks[ready]
            while (d, place) not in issued:
                communicate(1)
            take((d, place, 0))
            take((d, place, 1))
            unpack(place, d, ready * BLOCK)
            ready += 1
        when = steps[k] if k < len(steps) else {}
        attend(loader(chunk), k == 0, False, lambda t: communicate(when.get(t, 0)))
        if k == 0:
            suffix()
    for copy in w_copies:
        copy.wait_recv()
    for h in range(heads):
        rows = slice(h * SUF, (h + 1) * SUF)
        share = 1.0 / jnp.sum(sum_ref[rows, :], axis=1, keepdims=True)
        mixed = (acc_ref[rows, :] * share).astype(jnp.bfloat16)
        out_ref[:, h * VHEAD:(h + 1) * VHEAD] = jnp.dot(
            mixed, wg_ref[:, h].reshape(VLAT, VHEAD), preferred_element_type=jnp.float32
        ).astype(jnp.bfloat16)
    for copy in started:
        copy.wait_send()
    for condition, copies in guarded:
        @pl.when(condition)
        def _(copies=copies):
            for copy in copies:
                copy.wait_send()


def fused(n, serve_n, tables, length, *arrays):
    fresh, pages, queries, w = arrays
    depth = n // 4
    heads = queries.shape[1] // LAT
    raw = (fresh.shape[1] // LANES, LANES)
    dma = pltpu.SemaphoreType.DMA
    vmem = pl.BlockSpec(memory_space=pltpu.VMEM)
    hbm = pl.BlockSpec(memory_space=pltpu.HBM)
    bf16, f32, i32 = jnp.bfloat16, jnp.float32, jnp.int32
    rows = heads * SUF
    return pl.pallas_call(
        functools.partial(fused_kernel, n, serve_n),
        out_shape=(
            jax.ShapeDtypeStruct((SUF, heads * VHEAD), bf16),
            jax.ShapeDtypeStruct(pages.shape, bf16),
        ),
        in_specs=[hbm] * len(tables) + [pl.BlockSpec(memory_space=pltpu.SMEM)] + [hbm] * 4,
        out_specs=(vmem, vmem),
        scratch_shapes=[pltpu.SMEM(table.shape, i32) for table in tables] + [
            pltpu.VMEM(tables[0].shape, i32),
            pltpu.VMEM(fresh.shape, bf16),
            pltpu.VMEM(pages.shape, bf16),
            pltpu.VMEM((FLAT * SHELF, LANES), f32),
            pltpu.VMEM((HOT * FLAT, LANES), f32),
            pltpu.VMEM(raw, f32),
            pltpu.VMEM(raw, bf16),
            pltpu.VMEM(queries.shape, bf16),
            pltpu.VMEM(w.shape, bf16),
            pltpu.VMEM((serve_n,) + w.shape, bf16),
            pltpu.VMEM((rows, WIDE), bf16),
            pltpu.VMEM((depth, 4, BLOCK, VLAT), bf16),
            pltpu.VMEM((depth, 4, BLOCK // 2, LANES), bf16),
            pltpu.VMEM((n * BLOCK, LANES), bf16),
            pltpu.VMEM((n,) + raw, bf16),
            pltpu.VMEM((n * raw[0], LANES), f32),
            pltpu.VMEM((SUF, WIDE), bf16),
            pltpu.VMEM((HOT, n, LANES), f32),
            pltpu.VMEM((2, TILE, 12 * PAGE), f32),
            pltpu.VMEM((rows, VLAT), f32),
            pltpu.VMEM((rows, LANES), f32),
            pltpu.VMEM((rows, LANES), f32),
            dma((9,)),
            dma((depth, 2, 2)), dma((depth, 2, 2)),
            dma((depth, 3, 2)), dma((depth, 3, 2)),
            dma((depth, 3, 2)), dma((depth, 3, 2)),
            dma((2, 2, 2)),
            dma((serve_n,)), dma((serve_n,)),
            dma((depth,)), dma((depth,)),
            dma((depth, 3)), dma((depth, 3)),
        ],
        compiler_params=pltpu.CompilerParams(
            collective_id=0, has_side_effects=True, vmem_limit_bytes=36 * 1024 * 1024
        ),
        name="fused",
    )(*(pltpu.with_memory_space_constraint(t, pltpu.HBM) for t in tables), length,
      *(pltpu.with_memory_space_constraint(t, pltpu.HBM) for t in arrays))


def local(n, serve_n, queries, new_latent, pool, page_owner, page_slot, new_owner, new_slot,
          prefix_len, w_uv):
    tables = (page_owner, page_slot, new_owner, new_slot)
    attended, updated = fused(n, serve_n, tables, prefix_len, new_latent, pool[0], queries[0], w_uv)
    return (attended[None], updated[None])


def solution(mesh):
    in_specs = (
        P("serve", None, "pool"),
        P("serve", "pool"),
        P("serve", "pool", None),
        P("serve", None),
        P("serve", None),
        P("serve", None),
        P("serve", None),
        P("serve"),
        P("pool", "serve", None),
    )
    out_specs = (P("serve", None, "pool"), P("serve", "pool", None))
    body = functools.partial(local, mesh.shape["pool"], mesh.shape["serve"])
    return jax.shard_map(body, mesh=mesh, in_specs=in_specs, out_specs=out_specs, check_vma=False)
```

time: 70.2 us -> 52 us (0.74)
  Pallas kernels: 60.3 us -> 48.7 us
  local copies, waits for them, and re-layouts: 6.72 us -> 1.81 us
  other arithmetic: 1.47 us -> 0 us
    pallas_call x1, Pallas kernels: 60.3 us -> 48.7 us  [fused(): pl.pallas_call(functools.partial(fused_kernel, n, serve_n), out_shape=(ja...]
    unnamed x2, local copies, waits for them, and re-layouts: 4.23 us -> 1.81 us
    unnamed x1 -> x0, other arithmetic: 1.47 us -> none
    concatenate x1 -> x0, local copies, waits for them, and re-layouts: 1.3 us -> none  [local(): jnp.concatenate([page_owner[0], page_slot[0], new_owner[0], new_slot[0],...]
    pad x1 -> x0, local copies, waits for them, and re-layouts: 1.2 us -> none  [local(): jnp.pad(page_owner, ((0, 0), (0, LANES - PPAGES)), constant_values=-1)]
where the time goes in v2:
time: 52 us; the launch traced here: 51.8 us
  Pallas kernels  48.7 us (94%)
  local copies, waits for them, and re-layouts  1.81 us (3%)
  between operations  1.29 us (2%)
    pallas_call x1, Pallas kernels, fused(): pl.pallas_call(functools.partial(fused_kernel, n, serve_n), out_shape=(ja...  48.7 us
    unnamed x2, local copies, waits for them, and re-layouts  1.81 us

profile of v2, /device:TPU:18, one launch (start us, length us, event | category | flops | bytes accessed | tf_op | source)
XLA Modules:
  0.0 51.8 jit_solution(12939269569000281931)
XLA Ops:
  1.3 48.7 %fused.1 = (bf16[256,1024]{1,0:T(8,128)(2,1)S(1)}, bf16[12,36864]{1,0:T(8,128)(2,1)S(1)}) custom-call(s32[1,32]{1,0:T(1,128)} %owner_hbm.1, s32[1,32]{1,0:T(1,128)} %slot_hbm.1, s32[1,4]{1,0:T(1,128)} %new_owner_hbm.1, s32[1,4]{1,0:T(1,128)} %new_slot_hbm.1, s32[1]{0:T(128)S(6)} %copy.13.len_ref, bf16[1,9216]{1,0:T(2,128)(2,1)} %fresh_hbm.1, ...), custom_call_target="tpu_custom_call" | custom-call | tf_op jit(solution)/shard_map/fused/pallas_call | solution.py:494
  50.0 0.8 %copy.14 = bf16[1,256,1024]{2,1,0:T(8,128)(2,1)} copy(bf16[1,256,1024]{2,1,0:T(8,128)(2,1)S(1)} %bitcast.5) | data formatting | bytes 1048576
  50.8 1.0 %copy.15 = bf16[1,12,36864]{2,1,0:T(8,128)(2,1)} copy(bf16[1,12,36864]{2,1,0:T(8,128)(2,1)S(1)} %bitcast.4) | data formatting | bytes 1769472

commit v3 on v2

--- a/solution.py
+++ b/solution.py
@@ -118,17 +118,15 @@
         parts, odd, _ = halves(flat_ref, r * FLAT, PAIR, lane)
         for c in range(4):
             at = slice(c * LANES, (c + 1) * LANES)
-            lat_ref[0, 0, r * PAGE:r * PAGE + PAIR, at] = parts[c].astype(jnp.bfloat16)
-            lat_ref[0, 0, r * PAGE + PAIR:(r + 1) * PAGE, at] = odd[c].astype(jnp.bfloat16)
-        rope_ref[0, 0, r * PAIR:(r + 1) * PAIR, :] = jnp.where(
+            lat_ref[z, 0, r * PAGE:r * PAGE + PAIR, at] = parts[c].astype(jnp.bfloat16)
+            lat_ref[z, 0, r * PAGE + PAIR:(r + 1) * PAGE, at] = odd[c].astype(jnp.bfloat16)
+        rope_ref[z, 0, r * PAIR:(r + 1) * PAIR, :] = jnp.where(
             lane < ROPE, parts[4], parts[8]).astype(jnp.bfloat16)
 
     fetches[3].wait()
     for k in range(raw_rows):
         own_ref[k:k + 1, :] = fresh_ref[:, k * LANES:(k + 1) * LANES].astype(jnp.float32)
     raw_ref[...] = own_ref[...].astype(jnp.bfloat16)
-    fetches[4].wait()
-
     pl.semaphore_wait(barrier, len(peers) + serve_n - 1)
 
     started = []
@@ -142,55 +140,38 @@
         started.append(copy)
         return copy
 
-    order = []
-    for d in range(1, depth // 2 + 1):
-        order.append(d)
-        if depth - d != d:
-            order.append(depth - d)
+    order = list(range(1, depth))
     planes = [0] + order
-
-    def base_of(d):
-        return ((z - d + depth) % depth) * 4
+    short = jnp.where(2 * z < depth, z, depth - 1 - z)
+    long_side = jnp.where(2 * z < depth, 1, -1)
+    inner = (z > 0) & (z < depth - 1)
+    plane = {0: z}
+    near = {}
+    for j in order:
+        both = j <= 2 * short
+        gap = jnp.where(both, (j + 1) // 2, j - short)
+        side = jnp.where(both & (j % 2 == 0), -long_side, long_side)
+        plane[j] = z + side * gap
+        near[j] = gap == 1
 
     owners = {}
-    for d in planes:
-        base = base_of(d)
-        owners[d, 0] = base + y * 2 + x
-        owners[d, 1] = base + y * 2 + (1 - x)
-        owners[d, 2] = base + (1 - y) * 2 + x
-        owners[d, 3] = base + (1 - y) * 2 + (1 - x)
+    for j in planes:
+        base = plane[j] * 4
+        owners[j, 0] = base + y * 2 + x
+        owners[j, 1] = base + y * 2 + (1 - x)
+        owners[j, 2] = base + (1 - y) * 2 + x
+        owners[j, 3] = base + (1 - y) * 2 + (1 - x)
 
     def views(d, place, h):
         return (
-            lat_ref.at[d, place, pl.ds(h * BLOCK // 2, BLOCK // 2)],
-            rope_ref.at[d, place, pl.ds(h * BLOCK // 4, BLOCK // 4)],
+            lat_ref.at[plane[d], place, pl.ds(h * BLOCK // 2, BLOCK // 2)],
+            rope_ref.at[plane[d], place, pl.ds(h * BLOCK // 4, BLOCK // 4)],
         )
 
     arrivals = {}
     issued = {(0, 0)}
 
-    def pass_on(src, dst, h, sends, recvs, d, slot, there):
-        copies = []
-        for part, (a, b) in enumerate(zip(views(*src, h), views(*dst, h))):
-            copies.append(send(
-                a, b, sends.at[d, slot, part], recvs.at[d, slot, part], {"pool": there}))
-        arrivals[dst + (h,)] = copies
-        issued.add(dst)
-
-    def take(key):
-        for copy in arrivals.pop(key, ()):
-            copy.wait_recv()
-
-    def spread(d, h):
-        pass_on((d, 0), (d, 1), h, x_send, x_recv, d, h, x_peer)
-        pass_on((d, 0), (d, 2), 1 - h, y_send, y_recv, d, 1 - h, y_peer)
-
-    def start_if(condition, copies):
-        @pl.when(condition)
-        def _():
-            for copy in copies:
-                copy.start()
-        guarded.append((condition, copies))
+    guarded = []
 
     def halved(src, dst, there, sends, recvs):
         return [
@@ -201,32 +182,53 @@
             for part, (a, b) in enumerate(zip(src, dst))
         ]
 
-    guarded = []
-    near = {1: (z == 0, z < depth - 1), depth - 1: (z == depth - 1, z > 0)}
+    def launch(condition, copies):
+        if condition is None:
+            for copy in copies:
+                copy.start()
+            started.extend(copies)
+            return
+
+        @pl.when(condition)
+        def _():
+            for copy in copies:
+                copy.start()
+        guarded.append((condition, copies))
+
+    def pass_on(src, dst, h, sends, recvs, d, slot, there, condition=None):
+        copies = halved(views(*src, h), views(*dst, h), there,
+                        sends.at[plane[d], slot], recvs.at[plane[d], slot])
+        launch(condition, copies)
+        arrivals[dst + (h,)] = copies
+        issued.add(dst)
+
+    def take(key):
+        for copy in arrivals.pop(key, ()):
+            copy.wait_recv()
+
+    def spread(d, h):
+        pass_on((d, 0), (d, 1), h, x_send, x_recv, d, h, x_peer)
+        pass_on((d, 0), (d, 2), 1 - h, y_send, y_recv, d, 1 - h, y_peer)
 
     def forward(d):
         for place, h, there, sends, recvs in (
             (1, 0, y_peer, y_send, y_recv), (2, 1, x_peer, x_send, x_recv)
         ):
             take((d, place, h))
-            if d in near:
-                copies = halved(views(d, place, h), views(d, 3, h), there,
-                                sends.at[d, 2], recvs.at[d, 2])
-                start_if(near[d][0], copies)
-                arrivals[d, 3, h] = copies
-                issued.add((d, 3))
-            else:
-                pass_on((d, place), (d, 3), h, sends, recvs, d, 2, there)
+            pass_on((d, place), (d, 3), h, sends, recvs, d, 2, there,
+                    None if d == 0 else jnp.logical_not(near[d]))
+
+    hops = ((z + 1, z < depth - 1), (z - 1, z > 0))
 
     def cross():
-        for h, recvs in ((0, y_recv), (1, x_recv)):
-            take((0, 3, h))
-        for i, d in enumerate(near):
+        take((0, 3, 0))
+        take((0, 3, 1))
+        for i, (to, exists) in enumerate(hops):
             copies = []
             for h, recvs in ((0, y_recv), (1, x_recv)):
-                copies += halved(views(0, 3, h), views(d, 3, h), column[d],
-                                 c_send.at[i, h], recvs.at[d, 2])
-            start_if(near[d][1], copies)
+                copies += halved(views(0, 3, h), views(0, 3, h), to * 4 + y * 2 + x,
+                                 c_send.at[i, h], recvs.at[z, 2])
+            launch(exists, copies)
 
     raw_column = {
         d: send(raw_ref, raws_ref.at[me], rz_send.at[d], rz_recv.at[d], {"pool": column[d]})
@@ -234,35 +236,66 @@
     }
     for h in range(2):
         spread(0, h)
-    for d in order:
+    for i, (to, exists) in enumerate(hops):
+        copies = []
         for h in range(2):
-            copies = []
-            for part, (a, b) in enumerate(zip(views(0, 0, h), views(d, 0, h))):
-                copies.append(send(
-                    a, b, z_send.at[d, h, part], z_recv.at[d, h, part], {"pool": column[d]}))
-            arrivals[d, 0, h] = copies
-            issued.add((d, 0))
+            copies += halved(views(0, 0, h), views(0, 0, h), to * 4 + y * 2 + x,
+                             z_send.at[i, z, h], z_recv.at[z, h])
+        launch(exists, copies)
 
     raw_copies = []
 
     def pass_raw(d):
-        owner = owners[d, 0]
+        owner = column[(depth - d) % depth]
         src = raw_ref if d == 0 else raws_ref.at[owner]
         for i, there in enumerate((x_peer, y_peer, far_peer)):
             raw_copies.append(send(
                 src, raws_ref.at[owner], r_send.at[d, i], r_recv.at[d, i], {"pool": there}))
 
     pass_raw(0)
+    fetches[4].wait()
     w_copies = [
         send(w_ref, wg_ref.at[core], w_send.at[d], w_recv.at[d], {"serve": (core + d) % serve_n})
         for d in range(1, serve_n)
     ]
 
-    def advance(d):
-        take((d, 0, 0))
-        take((d, 0, 1))
+    def advance(d, condition):
+        up = plane[d] < z
+        to = jnp.where(up, z + 1, z - 1)
+        further = jnp.where(up, z + 1 < depth, z > 0)
+        relays = [
+            halved(views(d, 0, h), views(d, 0, h), to * 4 + y * 2 + x,
+                   z_send.at[jnp.where(up, 0, 1), plane[d], h], z_recv.at[plane[d], h])
+            for h in range(2)
+        ]
+        spreads = []
         for h in range(2):
-            spread(d, h)
+            for place, half, there, sends, recvs in (
+                (1, h, x_peer, x_send, x_recv), (2, 1 - h, y_peer, y_send, y_recv)
+            ):
+                copies = halved(views(d, 0, half), views(d, place, half), there,
+                                sends.at[plane[d], half], recvs.at[plane[d], half])
+                arrivals[d, place, half] = copies
+                spreads.append(copies)
+
+        @pl.when(condition)
+        def _():
+            for h in range(2):
+                for copy in relays[h]:
+                    copy.wait_recv()
+
+                @pl.when(further)
+                def _():
+                    for copy in relays[h]:
+                        copy.start()
+            for copies in spreads:
+                for copy in copies:
+                    copy.start()
+        guarded.append((condition, sum(spreads, [])))
+        guarded.append((condition & further, sum(relays, [])))
+
+    def both_done(d):
+        issued.update(((d, 0), (d, 1), (d, 2)))
 
     for fetch in fetches[6:]:
         fetch.wait()
@@ -298,7 +331,7 @@
 
     def unpack(place, d, at):
         for r in range(HOT):
-            rope = rope_ref[d, place, r * PAIR:(r + 1) * PAIR, :].astype(jnp.float32)
+            rope = rope_ref[plane[d], place, r * PAIR:(r + 1) * PAIR, :].astype(jnp.float32)
             count = count_ref[r, pl.ds(owners[d, place], 1), :]
             turned = pltpu.roll(rope, ROPE, 1)
             line = lax.broadcasted_iota(jnp.int32, (PAIR, LANES), 0).astype(jnp.float32)
@@ -312,18 +345,13 @@
         raw_column[d].wait_recv()
         pass_raw(d)
 
-    blocks = [(0, 0), (0, 1), (0, 2)]
-    for k, d in enumerate(order):
+    blocks = [(0, 0), (0, 1), (0, 2), (0, 3)]
+    for d in order[:-1]:
         blocks += [(d, 0), (d, 1), (d, 2)]
-        if k == 0:
-            blocks.append((0, 3))
-    blocks += [(d, 3) for d in order]
+    blocks += [(order[-1], 0)] + [(d, 3) for d in order[:-1]]
+    blocks += [(order[-1], 1), (order[-1], 2), (order[-1], 3)]
     pages = [(i, d, place, r) for i, (d, place) in enumerate(blocks) for r in range(HOT)]
-    total = len(pages)
-    cuts = [8]
-    while total - cuts[-1] > 16:
-        cuts.append(cuts[-1] + 12)
-    cuts += [cuts[-1] + (total - cuts[-1]) // 2, total]
+    cuts = sorted({len(pages)} | set(range(8, len(pages), 12)) | set(range(12, len(pages), 12)))
     chunks = [pages[a:b] for a, b in zip([0] + cuts[:-1], cuts)]
 
     tiles = heads * SUF // TILE
@@ -331,7 +359,7 @@
     def loader(chunk):
         def latents(first, count):
             return jnp.concatenate(
-                [lat_ref[d, place, r * PAGE:(r + 1) * PAGE, :]
+                [lat_ref[plane[d], place, r * PAGE:(r + 1) * PAGE, :]
                  for _, d, place, r in chunk[first // PAGE:(first + count) // PAGE]], axis=0)
 
         def keys(first, count):
@@ -350,8 +378,9 @@
     def score(t, load, slot):
         _, keys, size = load
         for at in range(0, size, SUB):
-            s_ref[slot, :, at:at + SUB] = lax.dot_general(
-                qs_ref[t * TILE:(t + 1) * TILE, :], keys(at, SUB), contract_last,
+            width = min(SUB, size - at)
+            s_ref[slot, :, at:at + width] = lax.dot_general(
+                qs_ref[t * TILE:(t + 1) * TILE, :], keys(at, width), contract_last,
                 preferred_element_type=jnp.float32,
             )
 
@@ -391,26 +420,26 @@
         sum_ref[rows, :] = added
         acc_ref[rows, :] = mixed
 
-    def attend(load, first, causal, between):
-        score(0, load, 0)
-        for t in range(tiles):
-            if t + 1 < tiles:
-                score(t + 1, load, (t + 1) % 2)
-            absorb(t, load, t % 2, first, causal)
-            between(t)
-
-    pending = [functools.partial(forward, 0)]
-    for k, d in enumerate(order):
-        pending.append(functools.partial(advance, d))
-        if k == 0:
-            pending.append(cross)
-        pending.append(functools.partial(forward, d))
+    def advance_inner(d):
+        advance(d, inner)
+
+    def advance_outer(d):
+        advance(d, jnp.logical_not(inner))
+        both_done(d)
+
+    def step(action, *places):
+        return [functools.partial(action, d) for d in places]
+
+    pending = step(forward, 0) + step(advance_inner, 1, 2) + step(advance_outer, 1) + [cross]
+    pending += step(advance_inner, *order[2:]) + step(advance_outer, 2) + step(forward, 1, 2)
+    for d in order[2:]:
+        pending += step(advance_outer, d) + step(forward, d)
 
     def communicate(steps):
         for _ in range(min(steps, len(pending))):
             pending.pop(0)()
 
-    def suffix():
+    def prepare_suffix():
         for copy in raw_copies:
             copy.wait_recv()
         for o in range(n):
@@ -425,8 +454,7 @@
             sfx_ref[half * SUF // 2:(half + 1) * SUF // 2, VLAT:] = jnp.where(
                 wide_lane < ROPE, values, 0.0).astype(jnp.bfloat16)
 
-        attend(suffix_loader(), False, True, lambda t: communicate(1) if t % 2 else None)
-
+    def write_page():
         page = jnp.int32(0)
         slot = jnp.int32(-1)
         for m in range(NEWP):
@@ -446,12 +474,26 @@
 
         lax.fori_loop(0, PAIR, write, 0)
 
-    steps = [{0: 1, 2: 1}, {3: 1}, {0: 1, 3: 1}]
-
-    communicate(1)
+    steps = [{1: 1, 3: 1}, {1: 1}, {1: 1}, {2: 2}, {}, {2: 1}]
+
+    def finish(t):
+        for h in range(t * TILE // SUF, (t + 1) * TILE // SUF):
+            rows = slice(h * SUF, (h + 1) * SUF)
+            share = 1.0 / jnp.sum(sum_ref[rows, :], axis=1, keepdims=True)
+            mixed = (acc_ref[rows, :] * share).astype(jnp.bfloat16)
+            out_ref[:, h * VHEAD:(h + 1) * VHEAD] = jnp.dot(
+                mixed, wg_ref[:, h].reshape(VLAT, VHEAD), preferred_element_type=jnp.float32
+            ).astype(jnp.bfloat16)
+
+    sequence = [0, -1] + list(range(1, len(chunks)))
     ready = 0
-    for k, chunk in enumerate(chunks):
-        while ready <= chunk[-1][0]:
+
+    def prepare(i):
+        nonlocal ready
+        if sequence[i] < 0:
+            prepare_suffix()
+            return
+        while ready <= chunks[sequence[i]][-1][0]:
             d, place = blocks[ready]
             while (d, place) not in issued:
                 communicate(1)
@@ -459,19 +501,28 @@
             take((d, place, 1))
             unpack(place, d, ready * BLOCK)
             ready += 1
-        when = steps[k] if k < len(steps) else {}
-        attend(loader(chunk), k == 0, False, lambda t: communicate(when.get(t, 0)))
-        if k == 0:
-            suffix()
-    for copy in w_copies:
-        copy.wait_recv()
-    for h in range(heads):
-        rows = slice(h * SUF, (h + 1) * SUF)
-        share = 1.0 / jnp.sum(sum_ref[rows, :], axis=1, keepdims=True)
-        mixed = (acc_ref[rows, :] * share).astype(jnp.bfloat16)
-        out_ref[:, h * VHEAD:(h + 1) * VHEAD] = jnp.dot(
-            mixed, wg_ref[:, h].reshape(VLAT, VHEAD), preferred_element_type=jnp.float32
-        ).astype(jnp.bfloat16)
+        if i + 1 == len(sequence):
+            for copy in w_copies:
+                copy.wait_recv()
+
+    loads = [suffix_loader() if k < 0 else loader(chunks[k]) for k in sequence]
+    communicate(4)
+    prepare(0)
+    score(0, loads[0], 0)
+    for i, load in enumerate(loads):
+        when = steps[i] if i < len(steps) else {}
+        for t in range(tiles):
+            if t + 1 < tiles:
+                score(t + 1, load, (t + 1) % 2)
+            elif i + 1 < len(loads):
+                prepare(i + 1)
+                score(0, loads[i + 1], 0)
+            absorb(t, load, t % 2, i == 0, sequence[i] < 0)
+            if i + 1 == len(loads):
+                finish(t)
+            communicate(when.get(t, 0))
+        if i == 2:
+            write_page()
     for copy in started:
         copy.wait_send()
     for condition, copies in guarded:
@@ -523,7 +574,7 @@
             pltpu.VMEM((rows, LANES), f32),
             pltpu.VMEM((rows, LANES), f32),
             dma((9,)),
-            dma((depth, 2, 2)), dma((depth, 2, 2)),
+            dma((2, depth, 2, 2)), dma((depth, 2, 2)),
             dma((depth, 3, 2)), dma((depth, 3, 2)),
             dma((depth, 3, 2)), dma((depth, 3, 2)),
             dma((2, 2, 2)),

time: 52 us -> 48.2 us (0.927)
  the two profiles are of different devices: /device:TPU:18 before, /device:TPU:0 now
where the time goes in v3:
time: 48.2 us; the launch traced here: 48.1 us
  Pallas kernels  45 us (93%)
  local copies, waits for them, and re-layouts  1.81 us (4%)
  between operations  1.29 us (3%)
    pallas_call x1, Pallas kernels, fused(): pl.pallas_call(functools.partial(fused_kernel, n, serve_n), out_shape=(ja...  45 us
    unnamed x2, local copies, waits for them, and re-layouts  1.81 us

profile of v3, /device:TPU:0, one launch (start us, length us, event | category | flops | bytes accessed | tf_op | source)
XLA Modules:
  0.0 48.1 jit_solution(14156102980841430254)
XLA Ops:
  1.3 45.0 %fused.1 = (bf16[256,1024]{1,0:T(8,128)(2,1)S(1)}, bf16[12,36864]{1,0:T(8,128)(2,1)S(1)}) custom-call(s32[1,32]{1,0:T(1,128)} %owner_hbm.1, s32[1,32]{1,0:T(1,128)} %slot_hbm.1, s32[1,4]{1,0:T(1,128)} %new_owner_hbm.1, s32[1,4]{1,0:T(1,128)} %new_slot_hbm.1, s32[1]{0:T(128)S(6)} %copy.13.len_ref, bf16[1,9216]{1,0:T(2,128)(2,1)} %fresh_hbm.1, ...), custom_call_target="tpu_custom_call" | custom-call | tf_op jit(solution)/shard_map/fused/pallas_call | solution.py:545
  46.3 0.8 %copy.14 = bf16[1,256,1024]{2,1,0:T(8,128)(2,1)} copy(bf16[1,256,1024]{2,1,0:T(8,128)(2,1)S(1)} %bitcast.5) | data formatting | bytes 1048576
  47.1 1.0 %copy.15 = bf16[1,12,36864]{2,1,0:T(8,128)(2,1)} copy(bf16[1,12,36864]{2,1,0:T(8,128)(2,1)S(1)} %bitcast.4) | data formatting | bytes 1769472
